TPU v7x, 32 devices: a whole 2x2x4 slice. The times are simulated.
32 devices in a mesh: row: 4 (over x, core), col: 8 (over z, y).
Axes of the slice: x: 2, y: 2, z: 4, core: 2. Of those that a mesh axis runs over, the one named last changes fastest.
Arguments:
- rows: bfloat16 [1024, 4096], P(('row', 'col')), may hold values from -6 to 6
- task_ids: int32 [1024], P(('row', 'col')), may hold values from 0 to 8, as said below
- task_embed: bfloat16 [8, 4096], replicated, may hold values from -6 to 6
- norm_gain: float32 [4, 4096], replicated, may hold values from 0.1 to 1.9
- layer_weight: bfloat16 [4, 4096, 4096], P(None, None, 'col'), may hold values from -0.09375 to 0.09375
Outputs:
- packed_out: bfloat16 [1024, 4096], P('row', 'col')
Inputs may be any that keep to these rules, and one draw needn't show every extreme that they name: `task_ids`: 8 marks an empty row, smaller values name a task.
All inputs are finite; a program needn't handle non-finite values.
Results may differ from a plain program's by a relative error of at most 0.008.
Values may be sent and summed in bfloat16 or wider, within the bound.
A program may use at most 128 MiB of HBM per device.

v0:
```python
import jax
import jax.numpy as jnp
from jax import lax
from jax.sharding import PartitionSpec as P

epsilon = 1e-06


def entering(part, axis, combine, identity):
    place = lax.axis_index(axis)
    gathered = lax.all_gather(part, axis)
    state = jnp.zeros_like(part) + jnp.asarray(identity, part.dtype)

    def one(hop, state):
        return combine(state, lax.dynamic_index_in_dim(gathered, hop, 0, False))

    return lax.fori_loop(0, place, one, state)


def add_counts(earlier, later):
    return earlier + later


def activate_rows(hidden, gain):
    total_rows = hidden.shape[0]
    width = hidden.shape[1]
    block_rows = min(512, total_rows)

    def one_block(block):
        values = block.astype(jnp.float32)
        inverse_rms = lax.rsqrt(jnp.mean(values * values, axis=1, keepdims=True) + epsilon)
        return jax.nn.silu(values * inverse_rms * gain[None, :]).astype(jnp.bfloat16)

    blocks = hidden.reshape(total_rows // block_rows, block_rows, width)
    return lax.map(one_block, blocks).reshape(total_rows, width)


def shards(rows, task_ids, task_embed, norm_gain, layer_weight):
    row_count = rows.shape[0]
    width = rows.shape[1]
    task_count = task_embed.shape[0]
    row_devices = lax.axis_size("row")
    col_devices = lax.axis_size("col")
    capacity = row_count // row_devices + task_count
    slots_group = row_count * col_devices
    task_range = jnp.arange(task_count, dtype=jnp.int32)
    member = (task_ids[:, None] == task_range[None, :]).astype(jnp.int32)
    counts = jnp.sum(member, axis=0)
    zero_counts = jnp.zeros_like(counts)
    before_col = entering(counts, "col", add_counts, zero_counts)
    row_total = lax.psum(counts, "col")
    before_row = entering(row_total, "row", add_counts, zero_counts)
    totals = lax.psum(row_total, "row")
    before = before_row + before_col
    task_base = jnp.cumsum(totals) - totals
    positions = jnp.arange(row_count, dtype=jnp.int32)
    earlier_mask = positions[None, :] < positions[:, None]
    same_task = task_ids[:, None] == task_ids[None, :]
    task_rank = jnp.sum((same_task & earlier_mask).astype(jnp.int32), axis=1)
    row_live = task_ids < task_count
    packed_pos = (
        jnp.sum(member * (task_base + before)[None, :], axis=1).astype(jnp.int32) + task_rank
    )
    target_row = packed_pos % row_devices
    slot_index = packed_pos // row_devices
    before_pos = packed_pos[None, :] < packed_pos[:, None]
    same_target = (target_row[:, None] == target_row[None, :]) & row_live[None, :]
    within = jnp.sum((same_target & before_pos).astype(jnp.int32), axis=1)
    send_at = jnp.where(row_live, target_row * capacity + within, -1)
    buffer_range = jnp.arange(row_devices * capacity, dtype=jnp.int32)
    select = buffer_range[:, None] == send_at[None, :]
    send_rows = jnp.dot(
        select.astype(jnp.bfloat16), rows, preferred_element_type=jnp.float32
    ).astype(jnp.bfloat16)
    send_rows = send_rows.reshape(row_devices, capacity, width)
    send_slots = jnp.sum(jnp.where(select, slot_index[None, :] + 1, 0), axis=1) - 1
    send_slots = send_slots.reshape(row_devices, capacity)
    got_rows, got_slots = (
        lax.all_to_all(send_rows, "row", split_axis=0, concat_axis=0, tiled=True),
        lax.all_to_all(send_slots, "row", split_axis=0, concat_axis=0, tiled=True),
    )
    got_rows = got_rows.reshape(row_devices * capacity, width)
    got_slots = got_slots.reshape(row_devices * capacity)
    slot_range = jnp.arange(slots_group, dtype=jnp.int32)
    piece_rows = lax.all_gather(got_rows, "col", axis=0, tiled=True)
    piece_slots = lax.all_gather(got_slots, "col", axis=0, tiled=True)
    safe_slots = jnp.where(piece_slots >= 0, piece_slots, slots_group).astype(jnp.int32)
    placed = (
        jnp.zeros((slots_group, width), jnp.bfloat16).at[safe_slots].set(piece_rows, mode="drop")
    )
    group_index = lax.axis_index("row")
    slot_pos = slot_range * row_devices + group_index
    in_task = (slot_pos[:, None] >= task_base[None, :]) & (
        slot_pos[:, None] < (task_base + totals)[None, :]
    )
    task_term = jnp.dot(
        in_task.astype(jnp.bfloat16), task_embed, preferred_element_type=jnp.float32
    )
    hidden = (placed.astype(jnp.float32) + task_term).astype(jnp.bfloat16)
    part_width = width // col_devices
    column = lax.axis_index("col") * part_width
    layers = layer_weight.shape[0]
    result = hidden
    for layer_index in range(layers):
        active = activate_rows(hidden, norm_gain[layer_index])
        update = jnp.dot(active, layer_weight[layer_index], preferred_element_type=jnp.float32)
        own_cols = lax.dynamic_slice_in_dim(hidden, column, part_width, 1).astype(jnp.float32)
        result = (own_cols + update).astype(jnp.bfloat16)
        if layer_index + 1 < layers:
            hidden = lax.all_gather(result, "col", axis=1, tiled=True)
    return result


def solution(mesh):
    return jax.shard_map(
        shards,
        mesh=mesh,
        in_specs=(P(("row", "col"), None), P(("row", "col")), P(), P(), P(None, None, "col")),
        out_specs=P("row", "col"),
        check_vma=False,
    )
```

profile of v0, /device:TPU:0, one launch (start us, length us, event | category | flops | bytes accessed | tf_op | source)
XLA Modules:
  0.0 303.9 jit_solution(6992512767991493794)
XLA Ops:
  6.5 0.8 convert_reduce_fusion.2
  7.4 0.9 convert_reduce_fusion.1
  8.9 1.3 dynamic-slice.5
  11.1 13.1 %all-reduce.3 = (s32[8]{0:T(128)S(1)}, s32[64]{0:T(128)S(1)}) all-reduce(s32[8]{0:T(128)S(1)} %convert_reduce_fusion.2, s32[64]{0:T(128)S(1)} %dynamic-update-slice.1), channel_id=1, replica_groups=mesh['row'=4,'col'=8] {'col'}, use_global_device_ids=true, to_apply=%region_1.2 | all-reduce | flops 72 | bytes 576 | tf_op jit(solution)/shard_map/psum | solution.py:51
  24.2 1.2 dynamic-slice.4
  26.4 4.9 %all-reduce.4 = (s32[8]{0:T(128)S(1)}, s32[32]{0:T(128)S(1)}) all-reduce(s32[8]{0:T(128)S(1)} %get-tuple-element.117, s32[32]{0:T(128)S(1)} %dynamic-update-slice), channel_id=1, replica_groups=mesh['row'=4,'col'=8] {'row'}, use_global_device_ids=true, to_apply=%region_2.3 | all-reduce | flops 40 | bytes 320 | tf_op jit(solution)/shard_map/psum | solution.py:53
  33.7 11.9 %all_to_all.11 = bf16[4,16,4096]{2,1,0:T(8,128)(2,1)} all-to-all(bf16[4,16,4096]{2,1,0:T(8,128)(2,1)S(1)} %bitcast.53), channel_id=1, replica_groups=mesh['row'=4,'col'=8] {'row'}, dimensions={0} | all-to-all | bytes 1048576 | tf_op jit(solution)/shard_map/all_to_all | solution.py:79
  46.3 3.2 %all-to-all-start = ((s32[4,1,16]{2,1,0:T(1,128)}), s32[4,1,16]{2,1,0:T(1,128)S(1)}, u32[]{:S(2)}, u32[]{:S(2)}) async-start(s32[4,1,16]{2,1,0:T(1,128)} %bitcast.6), calls=%async_computation | async-start | bytes 4096 | tf_op jit(solution)/shard_map/all_to_all | solution.py:80
  50.3 1.1 fusion.112
  51.3 1.9 all-to-all-done
  54.7 9.3 %all-reduce.2 = s32[512]{0:T(512)S(1)} all-reduce(s32[512]{0:T(512)S(1)} %dynamic-update-slice.2), channel_id=1, replica_groups=mesh['row'=4,'col'=8] {'col'}, use_global_device_ids=true, to_apply=%add.2 | all-reduce | flops 512 | bytes 4096
  64.0 52.0 %all-gather.7.cloned.1.call-done = bf16[512,4096]{1,0:T(8,128)(2,1)} async-done(((bf16[64,4096]{1,0:T(8,128)(2,1)}), bf16[512,4096]{1,0:T(8,128)(2,1)}) %all-gather.7.cloned.1.call-update) | async-done | bytes 4194320 | tf_op jit(solution)/shard_map/all_gather | solution.py:85
  116.0 8.2 %scatter_custom_fusion = bf16[256,4096]{1,0:T(8,128)(2,1)S(1)} fusion(s32[512]{0:T(512)S(1)} %compare_select_fusion, bf16[512,4096]{1,0:T(8,128)(2,1)} %all-gather.7.cloned.1.call-done, bf16[]{:T(256)} %constant.131.clone.1), kind=kCustom, calls=%fused_computation.74 | custom fusion | bytes 2097664 | tf_op jit(solution)/shard_map/scatter | solution.py:89
  124.3 1.0 fusion.1
  125.3 4.4 %fusion.92 = bf16[256,512]{1,0:T(8,128)(2,1)} fusion(bf16[4,4096,512]{2,1,0:T(8,128)(2,1)} %param.13, bf16[256,4096]{1,0:T(8,128)(2,1)S(1)} %get-tuple-element.130, f32[4096]{0:T(1024)S(1)} %bitcast.57, f32[256]{0:T(256)S(1)} %add_rsqrt_fusion.3, s32[]{:T(128)S(6)} %select_n.59), kind=kOutput, calls=%fused_computation.73 | convolution fusion | flops 1082523648 | bytes 6833156 | tf_op jit(solution)/shard_map/dot_general | solution.py:106
  129.9 48.8 %all-gather.9.cloned.1.call-done = bf16[256,4096]{1,0:T(8,128)(2,1)} async-done(((bf16[256,512]{1,0:T(8,128)(2,1)}), bf16[256,4096]{1,0:T(8,128)(2,1)}) %all-gather.9.cloned.1.call-update) | async-done | bytes 2097168 | tf_op jit(solution)/shard_map/all_gather | solution.py:110
  178.7 2.1 fusion.9
  180.8 5.0 %fusion.87 = bf16[256,512]{1,0:T(8,128)(2,1)} fusion(bf16[4,4096,512]{2,1,0:T(8,128)(2,1)} %param.13, bf16[256,4096]{1,0:T(8,128)(2,1)} %all-gather.9.cloned.1.call-done, f32[4096]{0:T(1024)S(1)} %bitcast.56, f32[256]{0:T(256)S(1)} %add_rsqrt_fusion.2, s32[]{:T(128)S(6)} %select_n.59), kind=kOutput, calls=%fused_computation.72 | convolution fusion | flops 1082523648 | bytes 6833156 | tf_op jit(solution)/shard_map/dot_general | solution.py:106
  185.8 48.6 %all-gather.11.cloned.1.call-done = bf16[256,4096]{1,0:T(8,128)(2,1)} async-done(((bf16[256,512]{1,0:T(8,128)(2,1)}), bf16[256,4096]{1,0:T(8,128)(2,1)}) %all-gather.11.cloned.1.call-update) | async-done | bytes 2097168 | tf_op jit(solution)/shard_map/all_gather | solution.py:110
  234.5 2.1 fusion.17
  236.6 5.0 %fusion.82 = bf16[256,512]{1,0:T(8,128)(2,1)} fusion(bf16[4,4096,512]{2,1,0:T(8,128)(2,1)} %param.13, bf16[256,4096]{1,0:T(8,128)(2,1)} %all-gather.11.cloned.1.call-done, f32[4096]{0:T(1024)S(1)} %bitcast.55, f32[256]{0:T(256)S(1)} %add_rsqrt_fusion.1, s32[]{:T(128)S(6)} %select_n.59), kind=kOutput, calls=%fused_computation.71 | convolution fusion | flops 1082523648 | bytes 6833156 | tf_op jit(solution)/shard_map/dot_general | solution.py:106
  241.6 48.8 %all-gather.13.cloned.1.call-done = bf16[256,4096]{1,0:T(8,128)(2,1)} async-done(((bf16[256,512]{1,0:T(8,128)(2,1)}), bf16[256,4096]{1,0:T(8,128)(2,1)}) %all-gather.13.cloned.1.call-update) | async-done | bytes 2097168 | tf_op jit(solution)/shard_map/all_gather | solution.py:110
  290.3 2.1 fusion.25
  292.4 5.0 %fusion.77 = bf16[256,512]{1,0:T(8,128)(2,1)} fusion(bf16[4,4096,512]{2,1,0:T(8,128)(2,1)} %param.13, bf16[256,4096]{1,0:T(8,128)(2,1)} %all-gather.13.cloned.1.call-done, f32[4096]{0:T(1024)S(1)} %bitcast.54, f32[256]{0:T(256)S(1)} %add_rsqrt_fusion, s32[]{:T(128)S(6)} %select_n.59), kind=kOutput, calls=%fused_computation.70 | convolution fusion | flops 1082523648 | bytes 6833156 | tf_op jit(solution)/shard_map/dot_general | solution.py:106
  (44 shorter events, 6.2 us)
Async XLA Ops:
  6.5 26.7 %copy-start = (bf16[32,4096]{1,0:T(8,128)(2,1)S(1)}, bf16[32,4096]{1,0:T(8,128)(2,1)}, u32[]{:S(2)}) copy-start(bf16[32,4096]{1,0:T(8,128)(2,1)} %param.9) | copy-start | bytes 786436
  6.5 117.7 %copy-start.1 = (bf16[8,4096]{1,0:T(8,128)(2,1)S(1)}, bf16[8,4096]{1,0:T(8,128)(2,1)}, u32[]{:S(2)}) copy-start(bf16[8,4096]{1,0:T(8,128)(2,1)} %param.11) | copy-start | bytes 196612
  6.5 109.5 %all-gather.7.cloned.1.call-start = ((), (), s32[]{:S(2)}) async-start(), calls=%async_computation.2 | async-start | bytes 4718592 | tf_op jit(solution)/shard_map/all_gather | solution.py:85
  46.3 6.9 %all-to-all-start = ((s32[4,1,16]{2,1,0:T(1,128)}), s32[4,1,16]{2,1,0:T(1,128)S(1)}, u32[]{:S(2)}, u32[]{:S(2)}) async-start(s32[4,1,16]{2,1,0:T(1,128)} %bitcast.6), calls=%async_computation | async-start | bytes 4096 | tf_op jit(solution)/shard_map/all_to_all | solution.py:80
  49.6 129.1 %all-gather.9.cloned.1.call-start = ((), (), s32[]{:S(2)}) async-start(), calls=%async_computation.3 | async-start | bytes 2359296 | tf_op jit(solution)/shard_map/all_gather | solution.py:110
  129.7 104.8 %all-gather.11.cloned.1.call-start = ((), (), s32[]{:S(2)}) async-start(), calls=%async_computation.4 | async-start | bytes 2359296 | tf_op jit(solution)/shard_map/all_gather | solution.py:110
  185.8 104.5 %all-gather.13.cloned.1.call-start = ((), (), s32[]{:S(2)}) async-start(), calls=%async_computation.5 | async-start | bytes 2359296 | tf_op jit(solution)/shard_map/all_gather | solution.py:110
Sparse Core Ops, SparseCore 0:
  45.7 70.2 all-gather.6
  129.8 48.8 all-gather.8
  185.9 48.5 all-gather.10
  241.7 48.5 all-gather.12
where the time goes:
time: 304 us
  waiting for transfers between devices  200 us (66%)
  blocking collectives  39.2 us (13%)
  matrix products  20.7 us (7%)
  between operations  15.1 us (5%)
  local copies, waits for them, and re-layouts  13.9 us (5%)
  other arithmetic  11.3 us (4%)
  starting transfers between devices  3.53 us (1%)
    all_gather x3, waiting for transfers between devices, shards(): hidden = lax.all_gather(result, 'col', axis=1, tiled=True)  146 us
    all_gather x1, waiting for transfers between devices, shards(): piece_rows = lax.all_gather(got_rows, 'col', axis=0, tiled=True)  52 us
    dot_general x4, matrix products, shards(): jnp.dot(active, layer_weight[layer_index], preferred_element_type=jnp.flo...  19.3 us
    psum x1, blocking collectives, shards(): row_total = lax.psum(counts, 'col')  13.1 us
    all_to_all x1, blocking collectives, shards(): lax.all_to_all(send_rows, 'row', split_axis=0, concat_axis=0, tiled=True)  11.9 us
    unnamed x1, blocking collectives  9.34 us
    scatter x1, local copies, waits for them, and re-layouts, shards(): jnp.zeros((slots_group, width), jnp.bfloat16).at[safe_slots]  8.22 us
    reduce_sum x3, other arithmetic, one_block(): jnp.mean(values * values, axis=1, keepdims=True) + epsilon  6.25 us
  transfers between devices with their start and end apart: 5, of which 5 were waited for; matrix products, arithmetic and copies ran while one was open for 1% of the time, Pallas kernels for 0%

commit v1 on v0

--- a/solution.py
+++ b/solution.py
@@ -4,6 +4,22 @@
 from jax.sharding import PartitionSpec as P
 
 epsilon = 1e-06
+
+
+def ring_gather(x, axis, dim):
+    ways, here, step = (lax.axis_size(axis), lax.axis_index(axis), x.shape[dim])
+    shape = [n * ways if d == dim else n for d, n in enumerate(x.shape)]
+    full = lax.dynamic_update_slice_in_dim(jnp.zeros(shape, x.dtype), x, here * step, axis=dim)
+    going_up = going_down = x
+    for far in range(1, ways // 2 + 1):
+        going_up = lax.ppermute(going_up, axis, [(d, (d + 1) % ways) for d in range(ways)])
+        full = lax.dynamic_update_slice_in_dim(full, going_up, (here - far) % ways * step, axis=dim)
+        if 2 * far < ways:
+            going_down = lax.ppermute(going_down, axis, [(d, (d - 1) % ways) for d in range(ways)])
+            full = lax.dynamic_update_slice_in_dim(
+                full, going_down, (here + far) % ways * step, axis=dim
+            )
+    return full
 
 
 def entering(part, axis, combine, identity):
@@ -82,7 +98,7 @@
     got_rows = got_rows.reshape(row_devices * capacity, width)
     got_slots = got_slots.reshape(row_devices * capacity)
     slot_range = jnp.arange(slots_group, dtype=jnp.int32)
-    piece_rows = lax.all_gather(got_rows, "col", axis=0, tiled=True)
+    piece_rows = ring_gather(got_rows, "col", 0)
     piece_slots = lax.all_gather(got_slots, "col", axis=0, tiled=True)
     safe_slots = jnp.where(piece_slots >= 0, piece_slots, slots_group).astype(jnp.int32)
     placed = (

time: 304 us -> 337 us (1.11)
  starting transfers between devices: 3.53 us -> 30.4 us
  blocking collectives: 39.2 us -> 26.4 us
  local copies, waits for them, and re-layouts: 13.9 us -> 23.2 us
  matrix products: 20.7 us -> 24.1 us
    ppermute x0 -> x7, waiting for transfers between devices: none -> 53.1 us  [the longest x3 39.1 us: ring_gather(): lax.ppermute(going_down, axis, [(d, (d - 1) % ways) for d in range(ways)])]
    all_gather x1 -> x0, waiting for transfers between devices: 52 us -> none  [shards(): piece_rows = lax.all_gather(got_rows, 'col', axis=0, tiled=True)]
    ppermute x0 -> x7, starting transfers between devices: none -> 23.6 us  [the longest x3 19.5 us: ring_gather(): lax.ppermute(going_down, axis, [(d, (d - 1) % ways) for d in range(ways)])]
    all_to_all x1 -> x0, blocking collectives: 11.9 us -> none  [shards(): lax.all_to_all(send_rows, 'row', split_axis=0, concat_axis=0, tiled=True)]
    dynamic_update_slice x0 -> x8, local copies, waits for them, and re-layouts: none -> 6.73 us  [the longest x4 3.37 us: ring_gather(): lax.dynamic_update_slice_in_dim(full, going_up, (here - far) % ways * ste...]
    all_to_all x0 -> x1, starting transfers between devices: none -> 3.47 us  [shards(): lax.all_to_all(send_rows, 'row', split_axis=0, concat_axis=0, tiled=True)]
    reduce_sum x3 -> x4, other arithmetic: 6.25 us -> 9.27 us  [one_block(): jnp.mean(values * values, axis=1, keepdims=True) + epsilon]
  transfers between devices with their start and end apart: 5 -> 12, of which waited for: 5 -> 7; matrix products, arithmetic and copies ran while one was open for 1% -> 5% of each run, Pallas kernels for 0% -> 0%
where the time goes in v1:
time: 337 us; the launch traced here: 336 us
  waiting for transfers between devices  203 us (60%)
  starting transfers between devices  30.4 us (9%)
  blocking collectives  26.4 us (8%)
  matrix products  24.1 us (7%)
  local copies, waits for them, and re-layouts  23.2 us (7%)
  between operations  15 us (4%)
  other arithmetic  14.3 us (4%)
    all_gather x3, waiting for transfers between devices, shards(): hidden = lax.all_gather(result, 'col', axis=1, tiled=True)  149 us
    ppermute x3, waiting for transfers between devices, ring_gather(): lax.ppermute(going_down, axis, [(d, (d - 1) % ways) for d in range(ways)])  39.1 us
    ppermute x3, starting transfers between devices, ring_gather(): lax.ppermute(going_down, axis, [(d, (d - 1) % ways) for d in range(ways)])  19.5 us
    dot_general x4, matrix products, shards(): jnp.dot(active, layer_weight[layer_index], preferred_element_type=jnp.flo...  19.3 us
    ppermute x4, waiting for transfers between devices, ring_gather(): lax.ppermute(going_up, axis, [(d, (d + 1) % ways) for d in range(ways)])  14 us
    psum x1, blocking collectives, shards(): row_total = lax.psum(counts, 'col')  13.1 us
    reduce_sum x4, other arithmetic, one_block(): jnp.mean(values * values, axis=1, keepdims=True) + epsilon  9.27 us
    unnamed x1, blocking collectives  8.46 us
  transfers between devices with their start and end apart: 12, of which 7 were waited for; matrix products, arithmetic and copies ran while one was open for 5% of the time, Pallas kernels for 0%

profile of v1, /device:TPU:0, one launch (start us, length us, event | category | flops | bytes accessed | tf_op | source)
XLA Modules:
  0.0 336.1 jit_solution(8455702424593576657)
XLA Ops:
  10.9 13.1 %all-reduce.3 = (s32[8]{0:T(128)S(1)}, s32[64]{0:T(128)S(1)}) all-reduce(s32[8]{0:T(128)S(1)} %convert_reduce_fusion.2, s32[64]{0:T(128)S(1)} %dynamic-update-slice.1), channel_id=1, replica_groups=mesh['row'=4,'col'=8] {'col'}, use_global_device_ids=true, to_apply=%region_1.2 | all-reduce | flops 72 | bytes 576 | tf_op jit(solution)/shard_map/psum | solution.py:67
  26.2 4.9 %all-reduce.4 = (s32[8]{0:T(128)S(1)}, s32[32]{0:T(128)S(1)}) all-reduce(s32[8]{0:T(128)S(1)} %get-tuple-element.117, s32[32]{0:T(128)S(1)} %dynamic-update-slice), channel_id=1, replica_groups=mesh['row'=4,'col'=8] {'row'}, use_global_device_ids=true, to_apply=%region_2.3 | all-reduce | flops 40 | bytes 320 | tf_op jit(solution)/shard_map/psum | solution.py:69
  33.8 3.2 all-to-all-start
  40.7 3.5 %all-to-all-start.1 = ((bf16[4,16,4096]{2,1,0:T(8,128)(2,1)}), bf16[4,16,4096]{2,1,0:T(8,128)(2,1)S(1)}, u32[]{:S(2)}, u32[]{:S(2)}) async-start(bf16[4,16,4096]{2,1,0:T(8,128)(2,1)} %bitcast.8), calls=%async_computation.1 | async-start | bytes 1048576 | tf_op jit(solution)/shard_map/all_to_all | solution.py:95
  44.2 3.6 %fusion.90 = f32[256,4096]{1,0:T(8,128)} fusion(bf16[8,4096]{1,0:T(8,128)(2,1)} %param.11, s32[256]{0:T(256)S(1)} %multiply_add_fusion, s32[8]{0:T(128)S(1)} %bitcast.57, s32[8]{0:T(128)S(1)} %get-tuple-element.126), kind=kOutput, calls=%fused_computation.81 | convolution fusion | flops 16783360 | bytes 4260928 | tf_op jit(solution)/shard_map/dot_general | solution.py:112
  49.3 8.5 %all-reduce.2 = s32[512]{0:T(512)S(1)} all-reduce(s32[512]{0:T(512)S(1)} %dynamic-update-slice.2), channel_id=1, replica_groups=mesh['row'=4,'col'=8] {'col'}, use_global_device_ids=true, to_apply=%add.2 | all-reduce | flops 512 | bytes 4096
  59.4 3.1 collective-permute-start.1
  62.5 2.5 broadcast_in_dim.71
  65.8 14.0 %collective-permute-done = bf16[64,4096]{1,0:T(8,128)(2,1)S(1)} collective-permute-done((bf16[64,4096]{1,0:T(8,128)(2,1)S(1)}, bf16[64,4096]{1,0:T(8,128)(2,1)S(1)}, u32[]{:S(2)}, u32[]{:S(2)}) %collective-permute-start) | collective-permute-done | bytes 524320 | tf_op jit(solution)/shard_map/ppermute | solution.py:15
  79.7 2.5 collective-permute-start.2
  82.2 12.9 %collective-permute-start.3 = (bf16[64,4096]{1,0:T(8,128)(2,1)S(1)}, bf16[64,4096]{1,0:T(8,128)(2,1)S(1)}, u32[]{:S(2)}, u32[]{:S(2)}) collective-permute-start(bf16[64,4096]{1,0:T(8,128)(2,1)S(1)} %collective-permute-done.1), channel_id=1, source_target_pairs={{0,7},{1,0},{2,1},{3,2},{4,3},{5,4},{6,5},{7,6},{8,15},{9,8},{10,9... | collective-permute-start | bytes 1572872 | tf_op jit(solution)/shard_map/ppermute | solution.py:18
  96.9 20.0 %collective-permute-done.3 = bf16[64,4096]{1,0:T(8,128)(2,1)S(1)} collective-permute-done((bf16[64,4096]{1,0:T(8,128)(2,1)S(1)}, bf16[64,4096]{1,0:T(8,128)(2,1)S(1)}, u32[]{:S(2)}, u32[]{:S(2)}) %collective-permute-start.3) | collective-permute-done | bytes 524320 | tf_op jit(solution)/shard_map/ppermute | solution.py:18
  116.8 3.4 %collective-permute-start.5 = (bf16[64,4096]{1,0:T(8,128)(2,1)S(1)}, bf16[64,4096]{1,0:T(8,128)(2,1)S(1)}, u32[]{:S(2)}, u32[]{:S(2)}) collective-permute-start(bf16[64,4096]{1,0:T(8,128)(2,1)S(1)} %collective-permute-done.3), channel_id=1, source_target_pairs={{0,7},{1,0},{2,1},{3,2},{4,3},{5,4},{6,5},{7,6},{8,15},{9,8},{10,9... | collective-permute-start | bytes 1572872 | tf_op jit(solution)/shard_map/ppermute | solution.py:18
  122.8 19.2 %collective-permute-done.5 = bf16[64,4096]{1,0:T(8,128)(2,1)S(1)} collective-permute-done((bf16[64,4096]{1,0:T(8,128)(2,1)S(1)}, bf16[64,4096]{1,0:T(8,128)(2,1)S(1)}, u32[]{:S(2)}, u32[]{:S(2)}) %collective-permute-start.5) | collective-permute-done | bytes 524320 | tf_op jit(solution)/shard_map/ppermute | solution.py:18
  143.6 8.4 %scatter_custom_fusion = bf16[256,4096]{1,0:T(8,128)(2,1)S(1)} fusion(s32[512]{0:T(512)S(1)} %compare_select_fusion, bf16[512,4096]{1,0:T(8,128)(2,1)} %constant_dynamic-update-slice_fusion, bf16[]{:T(256)} %constant.174.clone.1), kind=kCustom, calls=%fused_computation.71 | custom fusion | bytes 2097664 | tf_op jit(solution)/shard_map/scatter | solution.py:105
  152.0 3.0 fusion
  155.1 4.4 %add_convert_fusion.1 = bf16[256,512]{1,0:T(8,128)(2,1)} fusion(bf16[256,4096]{1,0:T(8,128)(2,1)S(1)} %get-tuple-element.122, s32[]{:T(128)S(6)} %select_n.128, bf16[4,4096,512]{2,1,0:T(8,128)(2,1)} %param.13, f32[4096]{0:T(1024)S(1)} %bitcast.56, f32[256]{0:T(256)S(1)} %add_rsqrt_fusion.3), kind=kOutput, calls=%fused_computation.73 | convolution fusion | flops 1082523648 | bytes 6833156 | tf_op jit(solution)/shard_map/dot_general | solution.py:122
  159.5 51.4 %all-gather.6.cloned.1.call-done = bf16[256,4096]{1,0:T(8,128)(2,1)} async-done(((bf16[256,512]{1,0:T(8,128)(2,1)}), bf16[256,4096]{1,0:T(8,128)(2,1)}) %all-gather.6.cloned.1.call-update) | async-done | bytes 2097168 | tf_op jit(solution)/shard_map/all_gather | solution.py:126
  210.9 2.1 fusion.8
  213.0 5.0 %fusion.81 = bf16[256,512]{1,0:T(8,128)(2,1)} fusion(bf16[4,4096,512]{2,1,0:T(8,128)(2,1)} %param.13, bf16[256,4096]{1,0:T(8,128)(2,1)} %all-gather.6.cloned.1.call-done, f32[4096]{0:T(1024)S(1)} %bitcast.55, f32[256]{0:T(256)S(1)} %add_rsqrt_fusion.2, s32[]{:T(128)S(6)} %select_n.128), kind=kOutput, calls=%fused_computation.70 | convolution fusion | flops 1082523648 | bytes 6833156 | tf_op jit(solution)/shard_map/dot_general | solution.py:122
  218.1 48.6 %all-gather.8.cloned.1.call-done = bf16[256,4096]{1,0:T(8,128)(2,1)} async-done(((bf16[256,512]{1,0:T(8,128)(2,1)}), bf16[256,4096]{1,0:T(8,128)(2,1)}) %all-gather.8.cloned.1.call-update) | async-done | bytes 2097168 | tf_op jit(solution)/shard_map/all_gather | solution.py:126
  268.8 5.0 %fusion.76 = bf16[256,512]{1,0:T(8,128)(2,1)} fusion(bf16[4,4096,512]{2,1,0:T(8,128)(2,1)} %param.13, bf16[256,4096]{1,0:T(8,128)(2,1)} %all-gather.8.cloned.1.call-done, f32[4096]{0:T(1024)S(1)} %bitcast.54, f32[256]{0:T(256)S(1)} %add_rsqrt_fusion.1, s32[]{:T(128)S(6)} %select_n.128), kind=kOutput, calls=%fused_computation.69 | convolution fusion | flops 1082523648 | bytes 6833156 | tf_op jit(solution)/shard_map/dot_general | solution.py:122
  273.8 48.8 %all-gather.10.cloned.1.call-done = bf16[256,4096]{1,0:T(8,128)(2,1)} async-done(((bf16[256,512]{1,0:T(8,128)(2,1)}), bf16[256,4096]{1,0:T(8,128)(2,1)}) %all-gather.10.cloned.1.call-update) | async-done | bytes 2097168 | tf_op jit(solution)/shard_map/all_gather | solution.py:126
  324.6 5.0 %fusion.71 = bf16[256,512]{1,0:T(8,128)(2,1)} fusion(bf16[4,4096,512]{2,1,0:T(8,128)(2,1)} %param.13, bf16[256,4096]{1,0:T(8,128)(2,1)} %all-gather.10.cloned.1.call-done, f32[4096]{0:T(1024)S(1)} %bitcast.53, f32[256]{0:T(256)S(1)} %add_rsqrt_fusion, s32[]{:T(128)S(6)} %select_n.128), kind=kOutput, calls=%fused_computation.68 | convolution fusion | flops 1082523648 | bytes 6833156 | tf_op jit(solution)/shard_map/dot_general | solution.py:122
  (64 shorter events, 25.3 us)
Async XLA Ops:
  6.5 30.5 %copy-start = (bf16[32,4096]{1,0:T(8,128)(2,1)S(1)}, bf16[32,4096]{1,0:T(8,128)(2,1)}, u32[]{:S(2)}) copy-start(bf16[32,4096]{1,0:T(8,128)(2,1)} %param.9) | copy-start | bytes 786436
  33.8 6.9 %all-to-all-start = ((s32[4,1,16]{2,1,0:T(1,128)}), s32[4,1,16]{2,1,0:T(1,128)S(1)}, u32[]{:S(2)}, u32[]{:S(2)}) async-start(s32[4,1,16]{2,1,0:T(1,128)} %bitcast.6), calls=%async_computation | async-start | bytes 4096 | tf_op jit(solution)/shard_map/all_to_all | solution.py:96
  40.7 17.0 %all-to-all-start.1 = ((bf16[4,16,4096]{2,1,0:T(8,128)(2,1)}), bf16[4,16,4096]{2,1,0:T(8,128)(2,1)S(1)}, u32[]{:S(2)}, u32[]{:S(2)}) async-start(bf16[4,16,4096]{2,1,0:T(8,128)(2,1)} %bitcast.8), calls=%async_computation.1 | async-start | bytes 1048576 | tf_op jit(solution)/shard_map/all_to_all | solution.py:95
  44.2 166.7 %all-gather.6.cloned.1.call-start = ((), (), s32[]{:S(2)}) async-start(), calls=%async_computation.2 | async-start | bytes 2359296 | tf_op jit(solution)/shard_map/all_gather | solution.py:126
  57.7 22.0 %collective-permute-start = (bf16[64,4096]{1,0:T(8,128)(2,1)S(1)}, bf16[64,4096]{1,0:T(8,128)(2,1)S(1)}, u32[]{:S(2)}, u32[]{:S(2)}) collective-permute-start(bf16[64,4096]{1,0:T(8,128)(2,1)S(1)} %bitcast.50), channel_id=1, source_target_pairs={{0,1},{1,2},{2,3},{3,4},{4,5},{5,6},{6,7},{7,0},{8,9},{9,10},{10,1... | collective-permute-start | bytes 1572872 | tf_op jit(solution)/shard_map/ppermute | solution.py:15
  59.4 22.9 %collective-permute-start.1 = (bf16[64,4096]{1,0:T(8,128)(2,1)S(1)}, bf16[64,4096]{1,0:T(8,128)(2,1)S(1)}, u32[]{:S(2)}, u32[]{:S(2)}) collective-permute-start(bf16[64,4096]{1,0:T(8,128)(2,1)S(1)} %bitcast.51), channel_id=1, source_target_pairs={{0,7},{1,0},{2,1},{3,2},{4,3},{5,4},{6,5},{7,6},{8,15},{9,8},{10,9... | collective-permute-start | bytes 1572872 | tf_op jit(solution)/shard_map/ppermute | solution.py:18
  79.7 17.1 %collective-permute-start.2 = (bf16[64,4096]{1,0:T(8,128)(2,1)S(1)}, bf16[64,4096]{1,0:T(8,128)(2,1)S(1)}, u32[]{:S(2)}, u32[]{:S(2)}) collective-permute-start(bf16[64,4096]{1,0:T(8,128)(2,1)S(1)} %collective-permute-done), channel_id=1, source_target_pairs={{0,1},{1,2},{2,3},{3,4},{4,5},{5,6},{6,7},{7,0},{8,9},{9,10},{10,1... | collective-permute-start | bytes 1572872 | tf_op jit(solution)/shard_map/ppermute | solution.py:15
  82.2 34.6 %collective-permute-start.3 = (bf16[64,4096]{1,0:T(8,128)(2,1)S(1)}, bf16[64,4096]{1,0:T(8,128)(2,1)S(1)}, u32[]{:S(2)}, u32[]{:S(2)}) collective-permute-start(bf16[64,4096]{1,0:T(8,128)(2,1)S(1)} %collective-permute-done.1), channel_id=1, source_target_pairs={{0,7},{1,0},{2,1},{3,2},{4,3},{5,4},{6,5},{7,6},{8,15},{9,8},{10,9... | collective-permute-start | bytes 1572872 | tf_op jit(solution)/shard_map/ppermute | solution.py:18
  96.9 25.0 %collective-permute-start.4 = (bf16[64,4096]{1,0:T(8,128)(2,1)S(1)}, bf16[64,4096]{1,0:T(8,128)(2,1)S(1)}, u32[]{:S(2)}, u32[]{:S(2)}) collective-permute-start(bf16[64,4096]{1,0:T(8,128)(2,1)S(1)} %collective-permute-done.2), channel_id=1, source_target_pairs={{0,1},{1,2},{2,3},{3,4},{4,5},{5,6},{6,7},{7,0},{8,9},{9,10},{10,1... | collective-permute-start | bytes 1572872 | tf_op jit(solution)/shard_map/ppermute | solution.py:15
  116.8 25.1 %collective-permute-start.5 = (bf16[64,4096]{1,0:T(8,128)(2,1)S(1)}, bf16[64,4096]{1,0:T(8,128)(2,1)S(1)}, u32[]{:S(2)}, u32[]{:S(2)}) collective-permute-start(bf16[64,4096]{1,0:T(8,128)(2,1)S(1)} %collective-permute-done.3), channel_id=1, source_target_pairs={{0,7},{1,0},{2,1},{3,2},{4,3},{5,4},{6,5},{7,6},{8,15},{9,8},{10,9... | collective-permute-start | bytes 1572872 | tf_op jit(solution)/shard_map/ppermute | solution.py:18
  121.9 20.9 %collective-permute-start.6 = (bf16[64,4096]{1,0:T(8,128)(2,1)S(1)}, bf16[64,4096]{1,0:T(8,128)(2,1)S(1)}, u32[]{:S(2)}, u32[]{:S(2)}) collective-permute-start(bf16[64,4096]{1,0:T(8,128)(2,1)S(1)} %collective-permute-done.4), channel_id=1, source_target_pairs={{0,1},{1,2},{2,3},{3,4},{4,5},{5,6},{6,7},{7,0},{8,9},{9,10},{10,1... | collective-permute-start | bytes 1572872 | tf_op jit(solution)/shard_map/ppermute | solution.py:15
  159.4 107.3 %all-gather.8.cloned.1.call-start = ((), (), s32[]{:S(2)}) async-start(), calls=%async_computation.3 | async-start | bytes 2359296 | tf_op jit(solution)/shard_map/all_gather | solution.py:126
  218.0 104.5 %all-gather.10.cloned.1.call-start = ((), (), s32[]{:S(2)}) async-start(), calls=%async_computation.4 | async-start | bytes 2359296 | tf_op jit(solution)/shard_map/all_gather | solution.py:126
Sparse Core Ops, SparseCore 0:
  159.5 51.3 all-gather.5
  218.1 48.5 all-gather.7
  273.9 48.5 all-gather.9
